TPU v7x, 32 devices: a whole 2x2x4 slice. The times are simulated.
32 devices in a mesh: level: 4 (over z), dev: 8 (over y, x, core).
Axes of the slice: x: 2, y: 2, z: 4, core: 2. Of those that a mesh axis runs over, the one named last changes fastest.
Arguments:
- fields: float32 [4, 128, 12, 128], P('level', 'dev'), may hold values from -6 to 6
- own_src: int32 [4, 128], P('level', 'dev'), may hold values from 0 to 15
- own_weight: bfloat16 [4, 128, 128, 128], P('level', 'dev'), may hold values from 0 to 1, as said below
- send_block: int32 [4, 8, 8, 2], P('level', 'dev'), may hold values from 0 to 15
- send_target: int32 [4, 8, 8, 2], P('level', 'dev'), may hold values from 0 to 15
- send_count: int32 [4, 8, 8], P('level', 'dev'), may hold values from 0 to 2, as said below
- send_weight: bfloat16 [4, 8, 8, 2, 128, 128], P('level', 'dev'), may hold values from 0 to 1, as said below
- left_block: int32 [4, 8, 4, 2], P('level', 'dev'), may hold values from 0 to 15
- left_target: int32 [4, 8, 4, 2], P('level', 'dev'), may hold values from 0 to 15
- left_count: int32 [4, 8, 4], P('level', 'dev'), may hold values from 0 to 2, as said below
- left_weight: bfloat16 [4, 8, 4, 2, 128, 128], P('level', 'dev'), may hold values from 0 to 1, as said below
Outputs:
- remapped: float32 [4, 128, 12, 128], P('level', 'dev')
- totals: float32 [12], replicated
Inputs may be any that keep to these rules, and one draw needn't show every extreme that they name: send_count[l, s, s] = 0; for every level some receiver device gets 2 live slots from every other device of the level. left_count[m, q, m] = 0; for every device index some receiver level gets 2 live slots from every other level. `own_weight`: nonnegative; entry [k, i] is zero where old cell k and new cell i differ by more than 3; each column sums to a positive intersect fraction of at most 1. `send_weight`: nonnegative; entry [k, i] is zero where old cell k and new cell i differ by more than 3; each column sums to a positive intersect fraction of at most 1. `left_weight`: nonnegative; entry [k, i] is zero where old cell k and new cell i differ by more than 3; each column sums to a positive intersect fraction of at most 1.
All inputs are finite; a program needn't handle non-finite values.
Results may differ from a plain program's by a relative error of at most 0.0045.
Values may be sent and summed in bfloat16 or wider, within the bound.
A program may use at most 64 MiB of HBM per device.

v0:
```python
import jax
import jax.numpy as jnp
from jax import lax
from jax.sharding import PartitionSpec as P


def pick_donors(rounded, block_index, count):
    donors = rounded[block_index]
    slots = block_index.shape[1]
    valid = lax.broadcasted_iota(jnp.int32, (1, slots), 1) < count[:, None]
    return jnp.where(valid[:, :, None, None], donors, jnp.zeros_like(donors))


def apply_weights(donors, weights):
    return jnp.einsum("pcmk,pcki->pcmi", donors, weights, preferred_element_type=jnp.float32)


def place_terms(contrib, target, blocks):
    comp = contrib.shape[2]
    cells = contrib.shape[3]
    flat_target = target.reshape(-1)
    onehot = (flat_target[:, None] == lax.broadcasted_iota(jnp.int32, (1, blocks), 1)).astype(
        jnp.float32
    )
    return jnp.einsum(
        "sb,smi->bmi", onehot, contrib.reshape(-1, comp, cells), precision=lax.Precision.HIGHEST
    )


def body(
    fields,
    own_src,
    own_weight,
    send_block,
    send_target,
    send_count,
    send_weight,
    left_block,
    left_target,
    left_count,
    left_weight,
):
    local = fields[0]
    blocks = local.shape[0]
    rounded = local.astype(jnp.bfloat16)
    own = jnp.einsum(
        "bmk,bki->bmi", rounded[own_src[0]], own_weight[0], preferred_element_type=jnp.float32
    )
    donors = pick_donors(rounded, send_block[0, 0], send_count[0, 0])
    strays = pick_donors(rounded, left_block[0, 0], left_count[0, 0])
    intra_terms, intra_target = (
        lax.all_to_all(
            apply_weights(donors, send_weight[0, 0]), "dev", split_axis=0, concat_axis=0, tiled=True
        ),
        lax.all_to_all(send_target[0, 0], "dev", split_axis=0, concat_axis=0, tiled=True),
    )
    left_terms, left_where = (
        lax.all_to_all(
            apply_weights(strays, left_weight[0, 0]),
            "level",
            split_axis=0,
            concat_axis=0,
            tiled=True,
        ),
        lax.all_to_all(left_target[0, 0], "level", split_axis=0, concat_axis=0, tiled=True),
    )
    remapped = (
        own
        + place_terms(intra_terms, intra_target, blocks)
        + place_terms(left_terms, left_where, blocks)
    )
    sums = lax.psum(jnp.sum(remapped, axis=(0, 2)), ("level", "dev"))
    totals = sums / (remapped.shape[2] * blocks)
    return (remapped[None], totals)


def solution(mesh):
    in_specs = (
        P("level", "dev", None, None),
        P("level", "dev"),
        P("level", "dev", None, None),
        P("level", "dev", None, None),
        P("level", "dev", None, None),
        P("level", "dev", None),
        P("level", "dev", None, None, None, None),
        P("level", "dev", None, None),
        P("level", "dev", None, None),
        P("level", "dev", None),
        P("level", "dev", None, None, None, None),
    )
    out_specs = (P("level", "dev", None, None), P())
    return jax.shard_map(body, mesh=mesh, in_specs=in_specs, out_specs=out_specs, check_vma=False)
```

profile of v0, /device:TPU:0, one launch (start us, length us, event | category | flops | bytes accessed | tf_op | source)
XLA Modules:
  0.0 84.1 jit_solution(18198775144529475194)
XLA Ops:
  0.7 0.7 copy-done.3
  1.4 0.6 copy.41
  2.0 6.3 %all-to-all-start.2 = ((s32[4,1,2]{2,1,0:T(1,128)}), s32[4,1,2]{2,1,0:T(1,128)S(1)}, u32[]{:S(2)}, u32[]{:S(2)}) async-start(s32[4,1,2]{2,1,0:T(1,128)} %copy.41), calls=%async_computation.2 | async-start | bytes 4096 | tf_op jit(solution)/shard_map/all_to_all | solution.py:65
  8.4 0.7 fusion.21
  9.0 0.7 iota_compare_fusion.3
  9.8 0.7 compare_select_fusion.1
  10.4 0.7 iota_compare_fusion.2
  11.2 0.7 compare_select_fusion
  12.2 1.3 %copy.36 = s32[8,1,2]{2,1,0:T(1,128)} copy(s32[8,1,2]{0,2,1:T(2,128)} %bitcast.53) | data formatting | bytes 128 | tf_op jit(solution)/shard_map/all_to_all | solution.py:55
  13.6 0.9 %copy.52 = bf16[1,16,12,128]{3,2,1,0:T(8,128)(2,1)S(1)} copy(f32[1,16,12,128]{3,1,2,0:T(8,128)} %param.11) | data formatting | bytes 147456 | tf_op args[0]
  14.5 0.6 gather_fusion.2
  15.1 0.6 gather_fusion.1
  15.6 0.2 fusion.4
  15.9 0.3 fusion.1
  16.2 3.7 %all-to-all-start = ((s32[8,1,2]{2,1,0:T(1,128)}), s32[8,1,2]{2,1,0:T(1,128)S(1)}, u32[]{:S(2)}, u32[]{:S(2)}) async-start(s32[8,1,2]{2,1,0:T(1,128)} %copy.36), calls=%async_computation | async-start | bytes 8192 | tf_op jit(solution)/shard_map/all_to_all | solution.py:55
  19.9 0.6 copy.43
  20.6 4.0 %all-to-all-done = s32[8,1,2]{2,1,0:T(1,128)S(1)} async-done(((s32[8,1,2]{2,1,0:T(1,128)}), s32[8,1,2]{2,1,0:T(1,128)S(1)}, u32[]{:S(2)}, u32[]{:S(2)}) %all-to-all-start) | async-done | bytes 96 | tf_op jit(solution)/shard_map/all_to_all | solution.py:55
  24.5 5.1 %all-to-all-start.3 = ((f32[4,2,12,128]{3,1,2,0:T(2,128)}), f32[4,2,12,128]{3,1,2,0:T(2,128)S(1)}, u32[]{:S(2)}, u32[]{:S(2)}) async-start(f32[4,2,12,128]{3,1,2,0:T(2,128)} %copy.43), calls=%async_computation.3 | async-start | bytes 98304 | tf_op jit(solution)/shard_map/all_to_all | solution.py:58
  29.6 0.6 gather_fusion
  30.2 0.7 copy.38
  30.9 0.5 broadcast.122
  31.4 0.7 reduce.6
  32.2 0.7 reduce.7
  32.9 2.4 %all-to-all-done.3 = f32[4,2,12,128]{3,1,2,0:T(2,128)S(1)} async-done(((f32[4,2,12,128]{3,1,2,0:T(2,128)}), f32[4,2,12,128]{3,1,2,0:T(2,128)S(1)}, u32[]{:S(2)}, u32[]{:S(2)}) %all-to-all-start.3) | async-done | bytes 49184 | tf_op jit(solution)/shard_map/all_to_all | solution.py:58
  35.3 3.4 %all-to-all-start.1 = ((f32[8,2,12,128]{3,1,2,0:T(2,128)}), f32[8,2,12,128]{3,1,2,0:T(2,128)S(1)}, u32[]{:S(2)}, u32[]{:S(2)}) async-start(f32[8,2,12,128]{3,1,2,0:T(2,128)} %copy.38), calls=%async_computation.1 | async-start | bytes 196608 | tf_op jit(solution)/shard_map/all_to_all | solution.py:52
  38.7 0.3 fusion.18
  39.0 4.8 %all-to-all-done.1 = f32[8,2,12,128]{3,1,2,0:T(2,128)S(1)} async-done(((f32[8,2,12,128]{3,1,2,0:T(2,128)}), f32[8,2,12,128]{3,1,2,0:T(2,128)S(1)}, u32[]{:S(2)}, u32[]{:S(2)}) %all-to-all-start.1) | async-done | bytes 98336 | tf_op jit(solution)/shard_map/all_to_all | solution.py:52
  43.9 0.2 fusion.14
  44.1 0.4 fusion.24
  44.4 38.5 %psum.7 = f32[12]{0:T(128)S(1)} all-reduce(f32[12]{0:T(128)S(1)} %get-tuple-element.8), channel_id=1, replica_groups=mesh['level'=4,'dev'=8] {'level','dev'}, use_global_device_ids=true, to_apply=%region_1.2 | all-reduce | flops 12 | bytes 96 | tf_op jit(solution)/shard_map/psum | solution.py:72
  82.9 0.5 broadcast_multiply_fusion
  83.4 0.7 copy.46
  (19 shorter events, 0.6 us)
Async XLA Ops:
  0.6 43.4 %copy-start = (bf16[1,16,128,128]{3,2,1,0:T(8,128)(2,1)S(1)}, bf16[1,16,128,128]{3,2,1,0:T(8,128)(2,1)}, u32[]{:S(2)}) copy-start(bf16[1,16,128,128]{3,2,1,0:T(8,128)(2,1)} %param.13) | copy-start | bytes 1572868
  0.6 0.7 copy-start.3
  0.7 15.0 %copy-start.2 = (bf16[1,1,4,2,128,128]{5,4,3,2,1,0:T(8,128)(2,1)S(1)}, bf16[1,1,4,2,128,128]{5,4,3,2,1,0:T(8,128)(2,1)}, u32[]{:S(2)}) copy-start(bf16[1,1,4,2,128,128]{5,4,3,2,1,0:T(8,128)(2,1)} %param.21) | copy-start | bytes 786436
  0.7 15.2 %copy-start.1 = (bf16[1,1,8,2,128,128]{5,4,3,2,1,0:T(8,128)(2,1)S(1)}, bf16[1,1,8,2,128,128]{5,4,3,2,1,0:T(8,128)(2,1)}, u32[]{:S(2)}) copy-start(bf16[1,1,8,2,128,128]{5,4,3,2,1,0:T(8,128)(2,1)} %param.17) | copy-start | bytes 1572868
  2.0 14.2 %all-to-all-start.2 = ((s32[4,1,2]{2,1,0:T(1,128)}), s32[4,1,2]{2,1,0:T(1,128)S(1)}, u32[]{:S(2)}, u32[]{:S(2)}) async-start(s32[4,1,2]{2,1,0:T(1,128)} %copy.41), calls=%async_computation.2 | async-start | bytes 4096 | tf_op jit(solution)/shard_map/all_to_all | solution.py:65
  16.2 8.3 %all-to-all-start = ((s32[8,1,2]{2,1,0:T(1,128)}), s32[8,1,2]{2,1,0:T(1,128)S(1)}, u32[]{:S(2)}, u32[]{:S(2)}) async-start(s32[8,1,2]{2,1,0:T(1,128)} %copy.36), calls=%async_computation | async-start | bytes 8192 | tf_op jit(solution)/shard_map/all_to_all | solution.py:55
  24.5 10.8 %all-to-all-start.3 = ((f32[4,2,12,128]{3,1,2,0:T(2,128)}), f32[4,2,12,128]{3,1,2,0:T(2,128)S(1)}, u32[]{:S(2)}, u32[]{:S(2)}) async-start(f32[4,2,12,128]{3,1,2,0:T(2,128)} %copy.43), calls=%async_computation.3 | async-start | bytes 98304 | tf_op jit(solution)/shard_map/all_to_all | solution.py:58
  35.3 8.5 %all-to-all-start.1 = ((f32[8,2,12,128]{3,1,2,0:T(2,128)}), f32[8,2,12,128]{3,1,2,0:T(2,128)S(1)}, u32[]{:S(2)}, u32[]{:S(2)}) async-start(f32[8,2,12,128]{3,1,2,0:T(2,128)} %copy.38), calls=%async_computation.1 | async-start | bytes 196608 | tf_op jit(solution)/shard_map/all_to_all | solution.py:52
where the time goes:
time: 84.7 us; the launch traced here: 84.1 us
  blocking collectives  38.5 us (45%)
  starting transfers between devices  18.5 us (22%)
  waiting for transfers between devices  11.2 us (13%)
  local copies, waits for them, and re-layouts  8.43 us (10%)
  other arithmetic  5.33 us (6%)
  matrix products  1.38 us (2%)
    psum x1, blocking collectives, body(): sums = lax.psum(jnp.sum(remapped, axis=(0, 2)), ('level', 'dev'))  38.5 us
    all_to_all x1, starting transfers between devices, body(): lax.all_to_all(left_target[0, 0], 'level', split_axis=0, concat_axis=0, t...  6.35 us
    all_to_all x1, starting transfers between devices, body(): lax.all_to_all(apply_weights(strays, left_weight[0, 0]), 'level', split_a...  5.09 us
    all_to_all x1, waiting for transfers between devices, body(): lax.all_to_all(apply_weights(donors, send_weight[0, 0]), 'dev', split_axi...  4.79 us
    all_to_all x1, waiting for transfers between devices, body(): lax.all_to_all(send_target[0, 0], 'dev', split_axis=0, concat_axis=0, til...  3.97 us
    all_to_all x1, starting transfers between devices, body(): lax.all_to_all(send_target[0, 0], 'dev', split_axis=0, concat_axis=0, til...  3.74 us
    all_to_all x1, starting transfers between devices, body(): lax.all_to_all(apply_weights(donors, send_weight[0, 0]), 'dev', split_axi...  3.36 us
    all_to_all x1, waiting for transfers between devices, body(): lax.all_to_all(apply_weights(strays, left_weight[0, 0]), 'level', split_a...  2.42 us
  transfers between devices with their start and end apart: 4, of which 3 were waited for; matrix products, arithmetic and copies ran while one was open for 14% of the time, Pallas kernels for 0%

commit v1 on v0

--- a/solution.py
+++ b/solution.py
@@ -2,6 +2,20 @@
 import jax.numpy as jnp
 from jax import lax
 from jax.sharding import PartitionSpec as P
+
+
+def time_routes_all(x_part, join_dim, matrix):
+    kept_arr = x_part.shape
+    even = x_part.reshape(
+        *kept_arr[:join_dim], matrix, kept_arr[join_dim] // matrix, *kept_arr[join_dim + 1 :]
+    )
+    return jnp.moveaxis(even, join_dim, 0)
+
+
+def choose_values(content, where_dim):
+    field_out = list(content.shape[1:])
+    field_out[where_dim] *= content.shape[0]
+    return jnp.moveaxis(content, 0, where_dim).reshape(field_out)
 
 
 def pick_donors(rounded, block_index, count):
@@ -40,6 +54,23 @@
     left_count,
     left_weight,
 ):
+
+    def _process_teams(work_x, mesh_dim, chunk, local_x):
+        opened = lax.axis_size(mesh_dim)
+        passed, mixed_arr = (opened, lax.axis_index(mesh_dim))
+        v_now = time_routes_all(work_x, chunk, passed)
+        xs_all = [v_now[mixed_arr]]
+        for u in range(1, passed):
+            carry_out = v_now[(mixed_arr + u) % passed]
+            xs_all.append(
+                lax.ppermute(
+                    carry_out, mesh_dim, perm=[(i0, (i0 + u) % passed) for i0 in range(passed)]
+                )
+            )
+        u1 = jnp.stack(xs_all, axis=0)
+        v_now = u1[(mixed_arr - jnp.arange(passed)) % passed]
+        return choose_values(v_now, local_x)
+
     local = fields[0]
     blocks = local.shape[0]
     rounded = local.astype(jnp.bfloat16)
@@ -55,13 +86,7 @@
         lax.all_to_all(send_target[0, 0], "dev", split_axis=0, concat_axis=0, tiled=True),
     )
     left_terms, left_where = (
-        lax.all_to_all(
-            apply_weights(strays, left_weight[0, 0]),
-            "level",
-            split_axis=0,
-            concat_axis=0,
-            tiled=True,
-        ),
+        _process_teams(apply_weights(strays, left_weight[0, 0]), "level", 0, 0),
         lax.all_to_all(left_target[0, 0], "level", split_axis=0, concat_axis=0, tiled=True),
     )
     remapped = (

time: 84.7 us -> 80.9 us (0.955)
  waiting for transfers between devices: 11.2 us -> 6.91 us
  blocking collectives: 38.5 us -> 40 us
  local copies, waits for them, and re-layouts: 8.43 us -> 7.48 us
    all_to_all x1 -> x0, starting transfers between devices: 5.09 us -> none  [body(): lax.all_to_all(apply_weights(strays, left_weight[0, 0]), 'level', split_a...]
    ppermute x0 -> x3, starting transfers between devices: none -> 5 us  [_process_teams(): lax.ppermute(carry_out, mesh_dim, perm=[(i0, (i0 + u) % passed) for i0 in...]
    all_to_all x1 -> x0, waiting for transfers between devices: 2.42 us -> none  [body(): lax.all_to_all(apply_weights(strays, left_weight[0, 0]), 'level', split_a...]
    psum x1, blocking collectives: 38.5 us -> 40 us  [body(): sums = lax.psum(jnp.sum(remapped, axis=(0, 2)), ('level', 'dev'))]
    all_to_all x1, waiting for transfers between devices: 4.79 us -> 3.47 us  [body(): lax.all_to_all(apply_weights(donors, send_weight[0, 0]), 'dev', split_axi...]
    unnamed x10 -> x14, local copies, waits for them, and re-layouts: 2.33 us -> 2.1 us
  transfers between devices with their start and end apart: 4 -> 6, of which waited for: 3 -> 2; matrix products, arithmetic and copies ran while one was open for 14% -> 13% of each run, Pallas kernels for 0% -> 0%
where the time goes in v1:
time: 80.9 us; the launch traced here: 80.4 us
  blocking collectives  40 us (49%)
  starting transfers between devices  18.4 us (23%)
  local copies, waits for them, and re-layouts  7.48 us (9%)
  waiting for transfers between devices  6.91 us (9%)
  other arithmetic  5.37 us (7%)
  matrix products  1.36 us (2%)
  between operations  0.82 us (1%)
    psum x1, blocking collectives, body(): sums = lax.psum(jnp.sum(remapped, axis=(0, 2)), ('level', 'dev'))  40 us
    all_to_all x1, starting transfers between devices, body(): lax.all_to_all(left_target[0, 0], 'level', split_axis=0, concat_axis=0, t...  6.35 us
    ppermute x3, starting transfers between devices, _process_teams(): lax.ppermute(carry_out, mesh_dim, perm=[(i0, (i0 + u) % passed) for i0 in...  5 us
    all_to_all x1, starting transfers between devices, body(): lax.all_to_all(send_target[0, 0], 'dev', split_axis=0, concat_axis=0, til...  3.72 us
    all_to_all x1, waiting for transfers between devices, body(): lax.all_to_all(apply_weights(donors, send_weight[0, 0]), 'dev', split_axi...  3.47 us
    all_to_all x1, waiting for transfers between devices, body(): lax.all_to_all(send_target[0, 0], 'dev', split_axis=0, concat_axis=0, til...  3.43 us
    all_to_all x1, starting transfers between devices, body(): lax.all_to_all(apply_weights(donors, send_weight[0, 0]), 'dev', split_axi...  3.36 us
    unnamed x14, local copies, waits for them, and re-layouts  2.1 us
  transfers between devices with their start and end apart: 6, of which 2 were waited for; matrix products, arithmetic and copies ran while one was open for 13% of the time, Pallas kernels for 0%

profile of v1, /device:TPU:0, one launch (start us, length us, event | category | flops | bytes accessed | tf_op | source)
XLA Modules:
  0.0 80.4 jit_solution(16269435124400279014)
XLA Ops:
  0.7 0.7 copy-done.4
  1.4 0.7 copy.41
  2.1 6.3 %all-to-all-start.2 = ((s32[4,1,2]{2,1,0:T(1,128)}), s32[4,1,2]{2,1,0:T(1,128)S(1)}, u32[]{:S(2)}, u32[]{:S(2)}) async-start(s32[4,1,2]{2,1,0:T(1,128)} %copy.41), calls=%async_computation.2 | async-start | bytes 4096 | tf_op jit(solution)/shard_map/all_to_all | solution.py:90
  8.4 0.7 iota_compare_fusion.3
  9.1 0.7 compare_select_fusion
  10.1 0.6 gather_fusion.2
  10.6 0.2 fusion.4
  10.9 3.9 %collective-permute-start.2 = (f32[1,2,12,128]{3,2,1,0:T(8,128)S(1)}, f32[1,2,12,128]{3,2,1,0:T(8,128)S(1)}, u32[]{:S(2)}, u32[]{:S(2)}) collective-permute-start(f32[1,2,12,128]{3,2,1,0:T(8,128)S(1)} %get-tuple-element.9), channel_id=1, source_target_pairs={{0,24},{8,0},{16,8},{24,16},{1,25},{9,1},{17,9},{25,17},{2,26},{10... | collective-permute-start | bytes 36872 | tf_op jit(solution)/shard_map/ppermute | solution.py:66
  14.8 1.1 %collective-permute-start = (f32[1,2,12,128]{3,2,1,0:T(8,128)S(1)}, f32[1,2,12,128]{3,2,1,0:T(8,128)S(1)}, u32[]{:S(2)}, u32[]{:S(2)}) collective-permute-start(f32[1,2,12,128]{3,2,1,0:T(8,128)S(1)} %get-tuple-element.11), channel_id=1, source_target_pairs={{0,8},{8,16},{16,24},{24,0},{1,9},{9,17},{17,25},{25,1},{2,10},{10... | collective-permute-start | bytes 36872 | tf_op jit(solution)/shard_map/ppermute | solution.py:66
  15.9 0.7 fusion.23
  16.6 0.7 compare_select_fusion.1
  17.3 0.7 iota_compare_fusion.2
  18.2 0.6 gather_fusion.1
  18.7 0.3 fusion.1
  19.1 0.7 copy-done.5
  19.7 0.7 copy.36
  20.4 0.6 gather_fusion
  21.0 0.7 copy.38
  21.7 3.7 %all-to-all-start = ((s32[8,1,2]{2,1,0:T(1,128)}), s32[8,1,2]{2,1,0:T(1,128)S(1)}, u32[]{:S(2)}, u32[]{:S(2)}) async-start(s32[8,1,2]{2,1,0:T(1,128)} %copy.36), calls=%async_computation | async-start | bytes 8192 | tf_op jit(solution)/shard_map/all_to_all | solution.py:86
  25.4 0.5 broadcast.194
  25.9 0.7 reduce.6
  26.7 3.4 %all-to-all-done = s32[8,1,2]{2,1,0:T(1,128)S(1)} async-done(((s32[8,1,2]{2,1,0:T(1,128)}), s32[8,1,2]{2,1,0:T(1,128)S(1)}, u32[]{:S(2)}, u32[]{:S(2)}) %all-to-all-start) | async-done | bytes 96 | tf_op jit(solution)/shard_map/all_to_all | solution.py:86
  30.1 3.4 %all-to-all-start.1 = ((f32[8,2,12,128]{3,1,2,0:T(2,128)}), f32[8,2,12,128]{3,1,2,0:T(2,128)S(1)}, u32[]{:S(2)}, u32[]{:S(2)}) async-start(f32[8,2,12,128]{3,1,2,0:T(2,128)} %copy.38), calls=%async_computation.1 | async-start | bytes 196608 | tf_op jit(solution)/shard_map/all_to_all | solution.py:83
  33.5 0.7 reduce.7
  34.3 0.6 gather_fusion.3
  34.8 0.3 fusion.9
  35.1 3.5 %all-to-all-done.1 = f32[8,2,12,128]{3,1,2,0:T(2,128)S(1)} async-done(((f32[8,2,12,128]{3,1,2,0:T(2,128)}), f32[8,2,12,128]{3,1,2,0:T(2,128)S(1)}, u32[]{:S(2)}, u32[]{:S(2)}) %all-to-all-start.1) | async-done | bytes 98336 | tf_op jit(solution)/shard_map/all_to_all | solution.py:83
  38.6 0.2 fusion.16
  38.8 0.4 fusion.27
  39.2 40.0 %psum.7 = f32[12]{0:T(128)S(1)} all-reduce(f32[12]{0:T(128)S(1)} %get-tuple-element.12), channel_id=1, replica_groups=mesh['level'=4,'dev'=8] {'level','dev'}, use_global_device_ids=true, to_apply=%region_1.2 | all-reduce | flops 12 | bytes 96 | tf_op jit(solution)/shard_map/psum | solution.py:97
  79.2 0.5 broadcast_multiply_fusion
  79.8 0.7 copy.45
  (30 shorter events, 0.7 us)
Async XLA Ops:
  0.6 38.2 %copy-start = (bf16[1,16,128,128]{3,2,1,0:T(8,128)(2,1)S(1)}, bf16[1,16,128,128]{3,2,1,0:T(8,128)(2,1)}, u32[]{:S(2)}) copy-start(bf16[1,16,128,128]{3,2,1,0:T(8,128)(2,1)} %param.13) | copy-start | bytes 1572868
  0.6 0.7 copy-start.4
  0.7 9.4 %copy-start.3 = (f32[1,16,12,128]{3,1,2,0:T(8,128)S(1)}, f32[1,16,12,128]{3,1,2,0:T(8,128)}, u32[]{:S(2)}) copy-start(f32[1,16,12,128]{3,1,2,0:T(8,128)} %param.11) | copy-start | bytes 294916
  0.7 10.0 %copy-start.2 = (bf16[1,1,4,2,128,128]{5,4,3,2,1,0:T(8,128)(2,1)S(1)}, bf16[1,1,4,2,128,128]{5,4,3,2,1,0:T(8,128)(2,1)}, u32[]{:S(2)}) copy-start(bf16[1,1,4,2,128,128]{5,4,3,2,1,0:T(8,128)(2,1)} %param.21) | copy-start | bytes 786436
  0.7 18.1 %copy-start.1 = (bf16[1,1,8,2,128,128]{5,4,3,2,1,0:T(8,128)(2,1)S(1)}, bf16[1,1,8,2,128,128]{5,4,3,2,1,0:T(8,128)(2,1)}, u32[]{:S(2)}) copy-start(bf16[1,1,8,2,128,128]{5,4,3,2,1,0:T(8,128)(2,1)} %param.17) | copy-start | bytes 1572868
  2.1 19.6 %all-to-all-start.2 = ((s32[4,1,2]{2,1,0:T(1,128)}), s32[4,1,2]{2,1,0:T(1,128)S(1)}, u32[]{:S(2)}, u32[]{:S(2)}) async-start(s32[4,1,2]{2,1,0:T(1,128)} %copy.41), calls=%async_computation.2 | async-start | bytes 4096 | tf_op jit(solution)/shard_map/all_to_all | solution.py:90
  10.9 23.3 %collective-permute-start.2 = (f32[1,2,12,128]{3,2,1,0:T(8,128)S(1)}, f32[1,2,12,128]{3,2,1,0:T(8,128)S(1)}, u32[]{:S(2)}, u32[]{:S(2)}) collective-permute-start(f32[1,2,12,128]{3,2,1,0:T(8,128)S(1)} %get-tuple-element.9), channel_id=1, source_target_pairs={{0,24},{8,0},{16,8},{24,16},{1,25},{9,1},{17,9},{25,17},{2,26},{10... | collective-permute-start | bytes 36872 | tf_op jit(solution)/shard_map/ppermute | solution.py:66
  14.8 19.5 %collective-permute-start.1 = (f32[1,2,12,128]{3,2,1,0:T(8,128)S(1)}, f32[1,2,12,128]{3,2,1,0:T(8,128)S(1)}, u32[]{:S(2)}, u32[]{:S(2)}) collective-permute-start(f32[1,2,12,128]{3,2,1,0:T(8,128)S(1)} %get-tuple-element.10), channel_id=1, source_target_pairs={{0,16},{8,24},{16,0},{24,8},{1,17},{9,25},{17,1},{25,9},{2,18},{10... | collective-permute-start | bytes 36872 | tf_op jit(solution)/shard_map/ppermute | solution.py:66
  14.8 19.5 %collective-permute-start = (f32[1,2,12,128]{3,2,1,0:T(8,128)S(1)}, f32[1,2,12,128]{3,2,1,0:T(8,128)S(1)}, u32[]{:S(2)}, u32[]{:S(2)}) collective-permute-start(f32[1,2,12,128]{3,2,1,0:T(8,128)S(1)} %get-tuple-element.11), channel_id=1, source_target_pairs={{0,8},{8,16},{16,24},{24,0},{1,9},{9,17},{17,25},{25,1},{2,10},{10... | collective-permute-start | bytes 36872 | tf_op jit(solution)/shard_map/ppermute | solution.py:66
  19.1 0.7 copy-start.5
  21.7 8.4 %all-to-all-start = ((s32[8,1,2]{2,1,0:T(1,128)}), s32[8,1,2]{2,1,0:T(1,128)S(1)}, u32[]{:S(2)}, u32[]{:S(2)}) async-start(s32[8,1,2]{2,1,0:T(1,128)} %copy.36), calls=%async_computation | async-start | bytes 8192 | tf_op jit(solution)/shard_map/all_to_all | solution.py:86
  30.1 8.5 %all-to-all-start.1 = ((f32[8,2,12,128]{3,1,2,0:T(2,128)}), f32[8,2,12,128]{3,1,2,0:T(2,128)S(1)}, u32[]{:S(2)}, u32[]{:S(2)}) async-start(f32[8,2,12,128]{3,1,2,0:T(2,128)} %copy.38), calls=%async_computation.1 | async-start | bytes 196608 | tf_op jit(solution)/shard_map/all_to_all | solution.py:83
